TPU v7x, 32 devices: a whole 2x2x4 slice. The times are simulated.
32 devices in a mesh: dp: 8 (over z, x), tensor: 4 (over y, core).
Axes of the slice: x: 2, y: 2, z: 4, core: 2. Of those that a mesh axis runs over, the one named last changes fastest.
Arguments:
- streams: bfloat16 [128, 4, 7168], P('dp', None, 'tensor'), may hold values from -12 to 12
- mix_weight: bfloat16 [24, 4, 7168], P(None, None, 'tensor'), may hold values from -0.0625 to 0.0625
- mix_bias: float32 [24], replicated, may hold values from -4 to 4
- gate_weight: bfloat16 [18432, 7168], P('dp', 'tensor'), may hold values from -0.0625 to 0.0625
- up_weight: bfloat16 [18432, 7168], P('dp', 'tensor'), may hold values from -0.0625 to 0.0625
- down_weight: bfloat16 [18432, 7168], P('dp', 'tensor'), may hold values from -0.046875 to 0.046875
Outputs:
- new_streams: bfloat16 [128, 4, 7168], P('dp', None, 'tensor')
All inputs are finite; a program needn't handle non-finite values.
Results may differ from a plain program's by a relative error of at most 0.006.
The roundings to bfloat16 on the way count: a program that leaves them out, or rounds other values in their place, can miss the bound.
Values may be sent and summed in bfloat16 or wider, within the bound.
A program may use at most 64 MiB of HBM per device.

v0:
```python
import jax
import jax.numpy as jnp
from jax import lax
from jax.sharding import PartitionSpec as P

D = 7168
ITERS = 20


epsilon = 1e-06


def normalize(sweep_index, matrix):
    matrix = matrix / jnp.sum(matrix, axis=2, keepdims=True)
    return matrix / jnp.sum(matrix, axis=1, keepdims=True)


def mixing(raw_logits, squares, mix_bias, stream_count):
    scale_inv = lax.rsqrt(squares / (stream_count * D) + epsilon)
    logits = raw_logits * scale_inv[:, None] + mix_bias[None, :]
    pre_gate = jax.nn.sigmoid(logits[:, :stream_count])
    post_gate = 2.0 * jax.nn.sigmoid(logits[:, stream_count : 2 * stream_count])
    matrix = jnp.exp(logits[:, 2 * stream_count :]).reshape(-1, stream_count, stream_count)
    matrix = lax.fori_loop(0, ITERS, normalize, matrix)
    return (pre_gate, post_gate, matrix)


def contract_last(weights, rows):
    return lax.dot_general(
        weights, rows, (((1,), (1,)), ((), ())), preferred_element_type=jnp.float32
    )


def per_device(streams, mix_weight, mix_bias, gate_weight, up_weight, down_weight):
    tok_rows, stream_count, width_local = streams.shape
    logit_count = mix_weight.shape[0]
    flat_rows = streams.reshape(tok_rows, stream_count * width_local)
    flat_weight = mix_weight.reshape(logit_count, stream_count * width_local)
    raw_logits = lax.dot_general(
        flat_rows, flat_weight, (((1,), (1,)), ((), ())), preferred_element_type=jnp.float32
    )
    stream_wide = streams.astype(jnp.float32)
    squares = jnp.sum(stream_wide * stream_wide, axis=(1, 2))
    total_logits, total_squares = lax.psum((raw_logits, squares), "tensor")
    pre_gate, post_gate, res_mix = mixing(total_logits, total_squares, mix_bias, stream_count)
    mlp_input = jnp.einsum(
        "ts,tsc->tc", pre_gate, stream_wide, precision=lax.Precision.HIGHEST
    ).astype(jnp.bfloat16)
    unit_local = gate_weight.shape[0]
    block_rows = lax.all_gather(mlp_input, "dp", axis=0, tiled=True)
    gate_part = contract_last(gate_weight, block_rows)
    up_part = contract_last(up_weight, block_rows)
    both_parts = jnp.concatenate((gate_part, up_part), axis=0)
    unit_share = lax.psum_scatter(both_parts, "tensor", scatter_dimension=1, tiled=True)
    hidden_share = (jax.nn.silu(unit_share[:unit_local]) * unit_share[unit_local:]).astype(
        jnp.bfloat16
    )
    hidden = lax.all_gather(hidden_share, "tensor", axis=1, tiled=True)
    mlp_out = lax.psum_scatter(
        lax.dot_general(
            hidden, down_weight, (((0,), (0,)), ((), ())), preferred_element_type=jnp.float32
        ),
        "dp",
        scatter_dimension=0,
        tiled=True,
    )
    mixed = jnp.einsum("tij,tjc->tic", res_mix, stream_wide, precision=lax.Precision.HIGHEST)
    mixed = mixed + post_gate[:, :, None] * mlp_out[:, None, :]
    return mixed.astype(jnp.bfloat16)


def solution(mesh):
    in_specs = (
        P("dp", None, "tensor"),
        P(None, None, "tensor"),
        P(),
        P("dp", "tensor"),
        P("dp", "tensor"),
        P("dp", "tensor"),
    )
    out_specs = P("dp", None, "tensor")
    return jax.shard_map(
        per_device, mesh=mesh, in_specs=in_specs, out_specs=out_specs, check_vma=False
    )
```

profile of v0, /device:TPU:0, one launch (start us, length us, event | category | flops | bytes accessed | tf_op | source)
XLA Modules:
  0.0 182.8 jit_solution(2058229806804568332)
XLA Ops:
  6.5 0.0 copy-start
  6.5 0.0 reduce-scatter.3.cloned.1.call-start
  6.5 1.2 multiply_reduce_fusion
  7.8 0.0 copy-done
  7.8 1.2 convolution_bitcast_fusion.2
  8.9 8.7 %all-reduce = (f32[16,24]{1,0:T(8,128)S(1)}, f32[16]{0:T(128)S(1)}) all-reduce(f32[16,24]{1,0:T(8,128)S(1)} %convolution_bitcast_fusion.2, f32[16]{0:T(128)S(1)} %multiply_reduce_fusion), channel_id=1, replica_groups=mesh['dp'=8,'tensor'=4] {'tensor'}, use_global_device_ids=true, to_apply=%region_0.0 | all-reduce | flops 400 | bytes 3200 | tf_op jit(solution)/shard_map/psum | solution.py:44
  17.6 0.0 copy-start.1
  17.7 0.9 multiply_add_fusion
  18.5 0.1 fusion.10
  18.6 1.6 fusion.11
  20.3 31.8 %all_gather.6 = bf16[128,1792]{1,0:T(8,128)(2,1)S(1)} all-gather(bf16[16,1792]{1,0:T(8,128)(2,1)S(1)} %bitcast.24), channel_id=1, replica_groups=mesh['dp'=8,'tensor'=4] {'dp'}, dimensions={0}, use_global_device_ids=true | all-gather | bytes 516096 | tf_op jit(solution)/shard_map/all_gather | solution.py:50
  52.1 6.1 %convolution_bitcast_fusion = f32[2304,128]{0,1:T(8,128)S(1)} fusion(bf16[128,1792]{1,0:T(8,128)(2,1)S(1)} %all_gather.6, bf16[2304,1792]{1,0:T(8,128)(2,1)} %param.12), kind=kOutput, calls=%fused_computation.2 | convolution fusion | flops 1056964608 | bytes 9895936 | tf_op jit(solution)/shard_map/dot_general | solution.py:29
  58.2 0.0 copy-done.1
  58.2 2.8 %convolution_bitcast_fusion.1 = f32[2304,128]{0,1:T(8,128)S(1)} fusion(bf16[128,1792]{1,0:T(8,128)(2,1)S(1)} %all_gather.6, bf16[2304,1792]{1,0:T(8,128)(2,1)S(1)} %copy-done.1), kind=kOutput, calls=%fused_computation.3 | convolution fusion | flops 1056964608 | bytes 9895936 | tf_op jit(solution)/shard_map/dot_general | solution.py:29
  61.0 1.7 pad_maximum_fusion
  62.7 0.0 reduce-scatter.3.cloned.1.call-update
  62.7 0.0 reduce-scatter.5.cloned.1.call-start
  62.7 0.1 slice_exponential_fusion
  62.8 0.1 copy.13
  62.9 32.5 %reduce-scatter.3.cloned.1.call-done = f32[4608,32]{0,1:T(8,128)} async-done(((f32[4608,128]{0,1:T(8,128)}), f32[4608,32]{0,1:T(8,128)}) %reduce-scatter.3.cloned.1.call-update) | async-done | bytes 589840 | tf_op jit(solution)/shard_map/reduce_scatter | solution.py:54
  95.4 1.1 fusion.2
  96.6 7.0 %all_gather.7 = bf16[2304,128]{0,1:T(8,128)(2,1)S(1)} all-gather(bf16[2304,32]{0,1:T(8,128)(2,1)S(1)} %fusion.2), channel_id=1, replica_groups=mesh['dp'=8,'tensor'=4] {'tensor'}, dimensions={1}, use_global_device_ids=true | all-gather | bytes 737280 | tf_op jit(solution)/shard_map/all_gather | solution.py:58
  103.5 0.0 copy-start.2
  103.5 5.6 %fusion.12 = f32[128,1792]{1,0:T(8,128)} fusion(bf16[2304,128]{0,1:T(8,128)(2,1)S(1)} %all_gather.7, bf16[2304,1792]{1,0:T(8,128)(2,1)} %param.13), kind=kOutput, calls=%fused_computation.27 | convolution fusion | flops 1056964608 | bytes 9764864 | tf_op jit(solution)/shard_map/dot_general | solution.py:60
  109.1 0.0 reduce-scatter.5.cloned.1.call-update
  109.1 1.5 while.10
  110.7 0.1 copy.14
  110.8 63.1 %reduce-scatter.5.cloned.1.call-done = f32[16,1792]{1,0:T(8,128)} async-done(((f32[128,1792]{1,0:T(8,128)}), f32[16,1792]{1,0:T(8,128)}) %reduce-scatter.5.cloned.1.call-update) | async-done | bytes 114704 | tf_op jit(solution)/shard_map/reduce_scatter | solution.py:59
  173.8 0.0 copy-done.2
  173.9 2.1 %fusion = bf16[16,4,1792]{2,1,0:T(4,128)(2,1)} fusion(f32[16,4,4]{2,1,0:T(4,128)S(1)} %copy.14, bf16[16,4,1792]{2,1,0:T(4,128)(2,1)S(1)} %copy-done.2, f32[16,1792]{1,0:T(8,128)} %reduce-scatter.5.cloned.1.call-done, f32[16,4]{1,0:T(8,128)S(1)} %get-tuple-element.26), kind=kOutput, calls=%fused_computation.6 | convolution fusion | flops 5849088 | bytes 574720 | tf_op jit(solution)/shard_map/tij,tjc->tic/dot_general | solution.py:67
  (62 shorter events, 1.2 us)
Async XLA Ops:
  6.5 1.2 copy-start
  6.5 88.9 %reduce-scatter.3.cloned.1.call-start = ((), (), s32[]{:S(2)}) async-start(), calls=%async_computation.2 | async-start | bytes 2949120 | tf_op jit(solution)/shard_map/reduce_scatter | solution.py:54
  17.6 40.6 %copy-start.1 = (bf16[2304,1792]{1,0:T(8,128)(2,1)S(1)}, bf16[2304,1792]{1,0:T(8,128)(2,1)}, u32[]{:S(2)}) copy-start(bf16[2304,1792]{1,0:T(8,128)(2,1)} %param.11) | copy-start | bytes 24772612
  62.7 111.2 %reduce-scatter.5.cloned.1.call-start = ((), (), s32[]{:S(2)}) async-start(), calls=%async_computation.3 | async-start | bytes 1032192 | tf_op jit(solution)/shard_map/reduce_scatter | solution.py:59
  103.5 70.3 %copy-start.2 = (bf16[16,4,1792]{2,1,0:T(4,128)(2,1)S(1)}, bf16[16,4,1792]{2,1,0:T(4,128)(2,1)}, u32[]{:S(2)}) copy-start(bf16[16,4,1792]{2,1,0:T(4,128)(2,1)} %param.8) | copy-start | bytes 688132
Sparse Core Ops, SparseCore 0:
  62.8 32.5 reduce-scatter.2
  109.3 64.5 reduce-scatter.4
where the time goes:
time: 183 us
  waiting for transfers between devices  95.6 us (52%)
  blocking collectives  47.5 us (26%)
  matrix products  19.4 us (11%)
  between operations  13.5 us (7%)
  other arithmetic  6.14 us (3%)
    reduce_scatter x1, waiting for transfers between devices, per_device(): lax.psum_scatter(lax.dot_general(hidden, down_weight, (((0,), (0,)), ((),...  63.1 us
    reduce_scatter x1, waiting for transfers between devices, per_device(): lax.psum_scatter(both_parts, 'tensor', scatter_dimension=1, tiled=True)  32.5 us
    all_gather x1, blocking collectives, per_device(): block_rows = lax.all_gather(mlp_input, 'dp', axis=0, tiled=True)  31.8 us
    dot_general x2, matrix products, contract_last(): lax.dot_general(weights, rows, (((1,), (1,)), ((), ())), preferred_elemen...  8.91 us
    psum x1, blocking collectives, per_device(): total_logits, total_squares = lax.psum((raw_logits, squares), 'tensor')  8.71 us
    all_gather x1, blocking collectives, per_device(): hidden = lax.all_gather(hidden_share, 'tensor', axis=1, tiled=True)  6.96 us
    dot_general x1, matrix products, per_device(): lax.dot_general(hidden, down_weight, (((0,), (0,)), ((), ())), preferred_...  5.59 us
  transfers between devices with their start and end apart: 2, of which 2 were waited for; matrix products, arithmetic and copies ran while one was open for 1% of the time, Pallas kernels for 0%

commit v1 on v0

--- a/solution.py
+++ b/solution.py
@@ -1,6 +1,11 @@
+import functools
+import math
+
 import jax
 import jax.numpy as jnp
 from jax import lax
+from jax.experimental import pallas as pl
+from jax.experimental.pallas import tpu as pltpu
 from jax.sharding import PartitionSpec as P
 
 D = 7168
@@ -69,6 +74,431 @@
     return mixed.astype(jnp.bfloat16)
 
 
+MESH = pl.DeviceIdType.MESH
+UNIT_CHUNK = 256
+COLUMN_CHUNK = 256
+PAIR = 2
+VMEM_BUDGET = 58 * 1024 * 1024
+
+
+def column(values, at):
+    return values[:, at : at + 1]
+
+
+def sigmoid(v):
+    return 1.0 / (1.0 + jnp.exp(-v))
+
+
+def layer_kernel(
+    plan,
+    s_ref,
+    mw_ref,
+    bias_ref,
+    gate_hbm,
+    up_hbm,
+    down_hbm,
+    out_ref,
+    gate_v,
+    up_v,
+    down_v,
+    part,
+    part_in,
+    post,
+    rows_all,
+    mixed,
+    sums,
+    pair_out,
+    pair_in,
+    pair_sum,
+    ring_out,
+    ring_in,
+    hidden,
+    prod,
+    cross_out,
+    cross_in,
+    cross_sum,
+    line_out,
+    line_in,
+    w_sem,
+    a_send,
+    a_recv,
+    bz_send,
+    bz_recv,
+    bx_send,
+    bx_recv,
+    c1_send,
+    c1_recv,
+    c2_send,
+    c2_recv,
+    c3_send,
+    c3_recv,
+    c4_send,
+    c4_recv,
+    d1_send,
+    d1_recv,
+    d2_send,
+    d2_recv,
+):
+    zs, ys, tensors, chunks, nc, columns, cc, width_all = plan
+    streams, tok, width = s_ref.shape
+    dp = lax.axis_index("dp")
+    tp = lax.axis_index("tensor")
+    z, x = lax.div(dp, PAIR), lax.rem(dp, PAIR)
+    y, core = lax.div(tp, PAIR), lax.rem(tp, PAIR)
+    x_peer = (z * PAIR + 1 - x, tp)
+    core_peer = (dp, y * PAIR + 1 - core)
+
+    def z_at(r):
+        return lax.rem(z + r + zs, zs)
+
+    def y_at(r):
+        return lax.rem(y + r + ys, ys)
+
+    def z_peer(r):
+        return (z_at(r) * PAIR + x, tp)
+
+    def y_peer(r):
+        return (dp, y_at(r) * PAIR + core)
+
+    def t_peer(r):
+        return (dp, lax.rem(tp + r, tensors))
+
+    def send(src, dst, ssem, rsem, peer):
+        return pltpu.make_async_remote_copy(
+            src_ref=src, dst_ref=dst, send_sem=ssem, recv_sem=rsem, device_id=peer, device_id_type=MESH
+        )
+
+    def weight_copy(k, which):
+        hbm, vmem = ((gate_hbm, gate_v), (up_hbm, up_v), (down_hbm, down_v))[which]
+        return pltpu.make_async_copy(hbm.at[pl.ds(k * nc, nc)], vmem.at[pl.ds(k * nc, nc)], w_sem.at[which, k])
+
+    def start_gate_up(k, _):
+        weight_copy(k, 0).start()
+        weight_copy(k, 1).start()
+        return 0
+
+    def start_down(k, _):
+        weight_copy(k, 2).start()
+        return 0
+
+    lax.fori_loop(0, chunks, start_gate_up, 0)
+    lax.fori_loop(0, chunks, start_down, 0)
+
+    barrier = pltpu.get_barrier_semaphore()
+    peers = [t_peer(r) for r in range(1, tensors)] + [x_peer] + [z_peer(r) for r in range(1, zs)]
+    for peer in peers:
+        pl.semaphore_signal(barrier, inc=1, device_id=peer, device_id_type=MESH)
+
+    raw = jnp.zeros((tok, mw_ref.shape[1]), jnp.float32)
+    squares = jnp.zeros((tok, 1), jnp.float32)
+    for j in range(streams):
+        raw += contract_last(s_ref[j], mw_ref[j])
+        wide = s_ref[j].astype(jnp.float32)
+        squares += jnp.sum(wide * wide, axis=1, keepdims=True)
+    part[0] = jnp.zeros((tok, part.shape[2]), jnp.float32)
+    part[0, :, : raw.shape[1]] = raw
+    part[1] = jnp.broadcast_to(squares, (tok, part.shape[2]))
+    pl.semaphore_wait(barrier, len(peers))
+
+    def a_copy(r):
+        return send(part, part_in.at[r - 1], a_send.at[r - 1], a_recv.at[r - 1], t_peer(r))
+
+    for r in range(1, tensors):
+        a_copy(r).start()
+    for r in range(1, tensors):
+        a_copy(r).wait_recv()
+    total = part[...]
+    for r in range(1, tensors):
+        total = total + part_in[r - 1]
+    scale_inv = lax.rsqrt(total[1] / width_all + epsilon)
+    logits = total[0] * scale_inv + bias_ref[...]
+    gates = sigmoid(logits)
+    mlp_input = column(gates, 0) * s_ref[0].astype(jnp.float32)
+    for j in range(1, streams):
+        mlp_input += column(gates, j) * s_ref[j].astype(jnp.float32)
+    rows_all[z] = mlp_input.astype(jnp.bfloat16)
+
+    def bz_copy(r):
+        return send(rows_all.at[z], rows_all.at[z], bz_send.at[r - 1], bz_recv.at[r - 1], z_peer(r))
+
+    def bx_copy(r):
+        at = z_at(-r)
+        return send(rows_all.at[at], rows_all.at[zs + at], bx_send.at[r], bx_recv.at[r], x_peer)
+
+    bx_copy(0).start()
+    for r in range(1, zs):
+        bz_copy(r).start()
+    for i in range(streams):
+        post[i] = jnp.broadcast_to(2.0 * column(gates, streams + i), (tok, post.shape[2]))
+
+    entries = jnp.exp(logits)
+    mat = tuple(column(entries, 2 * streams + at) for at in range(streams * streams))
+
+    def sweep(_, m):
+        m = list(m)
+        for i in range(streams):
+            total_row = m[i * streams]
+            for j in range(1, streams):
+                total_row = total_row + m[i * streams + j]
+            inv = 1.0 / total_row
+            for j in range(streams):
+                m[i * streams + j] = m[i * streams + j] * inv
+        for j in range(streams):
+            total_col = m[j]
+            for i in range(1, streams):
+                total_col = total_col + m[i * streams + j]
+            inv = 1.0 / total_col
+            for i in range(streams):
+                m[i * streams + j] = m[i * streams + j] * inv
+        return tuple(m)
+
+    order = sorted(range(1, zs), key=lambda r: min(r, zs - r))
+    for r in order:
+        send(rows_all.at[z], rows_all.at[z_at(-r)], bz_send.at[r - 1], bz_recv.at[r - 1], z_peer(r)).wait_recv()
+        bx_copy(r).start()
+    mat = lax.fori_loop(0, ITERS, sweep, mat)
+    for i in range(streams):
+        line = mat[i * streams] * s_ref[0].astype(jnp.float32)
+        for j in range(1, streams):
+            line += mat[i * streams + j] * s_ref[j].astype(jnp.float32)
+        mixed[i] = line
+
+    def bx_arrival(r):
+        at = z_at(-r)
+        return send(rows_all.at[at], rows_all.at[zs + at], bx_send.at[r], bx_recv.at[r], x_peer)
+
+    for r in range(zs):
+        bx_arrival(r).wait_recv()
+
+    tokens = PAIR * zs * tok
+    half = tokens // PAIR
+    quarter = half // ys
+    own_slot = core * ys + y
+
+    def c1_copy(k):
+        return send(pair_out.at[k], pair_in.at[k], c1_send.at[k], c1_recv.at[k], core_peer)
+
+    def c2_copy(k, r):
+        at = (k * (ys - 1)) + r - 1
+        return send(ring_out.at[at], ring_in.at[at], c2_send.at[at], c2_recv.at[at], y_peer(r))
+
+    def units(k):
+        return pl.ds(pl.multiple_of(k * nc, nc), nc)
+
+    def c3_copy(k, r):
+        at = (k * (ys - 1)) + r - 1
+        piece = hidden.at[own_slot, :, units(k)]
+        return send(piece, piece, c3_send.at[at], c3_recv.at[at], y_peer(r))
+
+    def c3_arrival(k, r):
+        at = (k * (ys - 1)) + r - 1
+        piece = hidden.at[core * ys + y_at(-r), :, units(k)]
+        return send(piece, piece, c3_send.at[at], c3_recv.at[at], y_peer(r))
+
+    def c4_copy(k, r):
+        at = k * ys + r
+        piece = hidden.at[core * ys + y_at(-r), :, units(k)]
+        return send(piece, piece, c4_send.at[at], c4_recv.at[at], core_peer)
+
+    def c4_arrival(k, r):
+        at = k * ys + r
+        piece = hidden.at[(1 - core) * ys + y_at(-r), :, units(k)]
+        return send(piece, piece, c4_send.at[at], c4_recv.at[at], core_peer)
+
+    def c_first(k):
+        weight_copy(k, 0).wait()
+        weight_copy(k, 1).wait()
+        rows = rows_all[...].reshape(tokens, width)
+        sums[k, :, :, :nc] = contract_last(rows, gate_v[pl.ds(k * nc, nc)]).reshape(PAIR, half, nc)
+        sums[k, :, :, nc:] = contract_last(rows, up_v[pl.ds(k * nc, nc)]).reshape(PAIR, half, nc)
+        pair_out[k] = sums[k, 1 - core].astype(jnp.bfloat16)
+        c1_copy(k).start()
+
+    def c_second(k):
+        c1_copy(k).wait_recv()
+        both = sums[k, core] + pair_in[k].astype(jnp.float32)
+        pair_sum[k] = both.reshape(ys, quarter, PAIR * nc)
+        for r in range(1, ys):
+            ring_out[k * (ys - 1) + r - 1] = pair_sum[k, y_at(r)].astype(jnp.bfloat16)
+            c2_copy(k, r).start()
+
+    def c_third(k):
+        both = pair_sum[k, y]
+        for r in range(1, ys):
+            c2_copy(k, r).wait_recv()
+            both = both + ring_in[k * (ys - 1) + r - 1].astype(jnp.float32)
+        gate, up = both[:, :nc], both[:, nc:]
+        hidden[own_slot, :, units(k)] = (gate / (1.0 + jnp.exp(-gate)) * up).astype(jnp.bfloat16)
+        for r in range(1, ys):
+            c3_copy(k, r).start()
+        c4_copy(k, 0).start()
+
+    def c_fourth(k):
+        for r in range(1, ys):
+            c3_arrival(k, r).wait_recv()
+            c4_copy(k, r).start()
+
+    def pipeline(count, stages):
+        last = max(lag for lag, _ in stages)
+
+        def step(t, _):
+            for lag, stage in stages:
+                @pl.when(jnp.logical_and(t >= lag, t < count + lag))
+                def _():
+                    stage(t - lag)
+
+            return 0
+
+        lax.fori_loop(0, count + last, step, 0)
+
+    pipeline(chunks, ((0, c_first), (2, c_second), (4, c_third), (6, c_fourth)))
+
+    def finish_c(k, _):
+        for r in range(ys):
+            c4_arrival(k, r).wait_recv()
+        weight_copy(k, 2).wait()
+        return 0
+
+    lax.fori_loop(0, chunks, finish_c, 0)
+
+    def d1_copy(n):
+        return send(cross_out.at[n], cross_in.at[n], d1_send.at[n], d1_recv.at[n], x_peer)
+
+    def d2_copy(n, r):
+        at = n * (zs - 1) + r - 1
+        return send(line_out.at[at], line_in.at[at], d2_send.at[at], d2_recv.at[at], z_peer(r))
+
+    def cols(n):
+        return pl.ds(pl.multiple_of(n * cc, cc), cc)
+
+    def d_first(n):
+        rows = hidden[...].reshape(tokens, hidden.shape[2])
+        product = jnp.dot(rows, down_v[:, cols(n)], preferred_element_type=jnp.float32)
+        prod[n] = product[:half]
+        cross_out[n] = product[half:].astype(jnp.bfloat16)
+        d1_copy(n).start()
+
+    def d_second(n):
+        d1_copy(n).wait_recv()
+        cross_sum[n] = (prod[n] + cross_in[n].astype(jnp.float32)).reshape(zs, tok, cc)
+        for r in range(1, zs):
+            line_out[n * (zs - 1) + r - 1] = cross_sum[n, z_at(r)].astype(jnp.bfloat16)
+            d2_copy(n, r).start()
+
+    def d_third(n):
+        mlp_out = cross_sum[n, z]
+        for r in range(1, zs):
+            d2_copy(n, r).wait_recv()
+            mlp_out = mlp_out + line_in[n * (zs - 1) + r - 1].astype(jnp.float32)
+        for i in range(streams):
+            out_ref[i, :, cols(n)] = (mixed[i, :, cols(n)] + column(post[i], 0) * mlp_out).astype(jnp.bfloat16)
+
+    pipeline(columns, ((0, d_first), (1, d_second), (3, d_third)))
+
+    for r in range(1, tensors):
+        a_copy(r).wait_send()
+    for r in range(1, zs):
+        bz_copy(r).wait_send()
+    for r in range(zs):
+        bx_copy(r).wait_send()
+
+    def drain_c(k, _):
+        c1_copy(k).wait_send()
+        for r in range(1, ys):
+            c2_copy(k, r).wait_send()
+            c3_copy(k, r).wait_send()
+        for r in range(ys):
+            c4_copy(k, r).wait_send()
+        return 0
+
+    def drain_d(n, _):
+        d1_copy(n).wait_send()
+        for r in range(1, zs):
+            d2_copy(n, r).wait_send()
+        return 0
+
+    lax.fori_loop(0, chunks, drain_c, 0)
+    lax.fori_loop(0, columns, drain_d, 0)
+
+
+def layer_scratch(zs, ys, tensors, tok, streams, width, units, nc, cc):
+    tokens = PAIR * zs * tok
+    half = tokens // PAIR
+    quarter = half // ys
+    chunks, columns = units // nc, width // cc
+    f32, bf16 = jnp.float32, jnp.bfloat16
+    lanes = 128
+    arrays = [
+        ((units, width), bf16),
+        ((units, width), bf16),
+        ((units, width), bf16),
+        ((2, tok, lanes), f32),
+        ((tensors - 1, 2, tok, lanes), f32),
+        ((streams, tok, lanes), f32),
+        ((PAIR * zs, tok, width), bf16),
+        ((streams, tok, width), f32),
+        ((chunks, PAIR, half, 2 * nc), f32),
+        ((chunks, half, 2 * nc), bf16),
+        ((chunks, half, 2 * nc), bf16),
+        ((chunks, ys, quarter, 2 * nc), f32),
+        ((chunks * (ys - 1), quarter, 2 * nc), bf16),
+        ((chunks * (ys - 1), quarter, 2 * nc), bf16),
+        ((PAIR * ys, quarter, units), bf16),
+        ((columns, half, cc), f32),
+        ((columns, half, cc), bf16),
+        ((columns, half, cc), bf16),
+        ((columns, zs, tok, cc), f32),
+        ((columns * (zs - 1), tok, cc), bf16),
+        ((columns * (zs - 1), tok, cc), bf16),
+    ]
+    both = lambda count: [(count,), (count,)]
+    sems = [(3, chunks)]
+    for count in (tensors - 1, zs - 1, zs, chunks, chunks * (ys - 1), chunks * (ys - 1), chunks * ys, columns, columns * (zs - 1)):
+        sems += both(count)
+    size = sum(math.prod(shape) * jnp.dtype(kind).itemsize for shape, kind in arrays)
+    return arrays, sems, size
+
+
+def fused(mesh, streams, mix_weight, mix_bias, gate_weight, up_weight, down_weight):
+    tok, stream_count, width = streams.shape
+    units = gate_weight.shape[0]
+    dps, tensors = mesh.shape["dp"], mesh.shape["tensor"]
+    zs, ys = dps // PAIR, tensors // PAIR
+    nc, cc = UNIT_CHUNK, COLUMN_CHUNK
+    arrays, sems, _ = layer_scratch(zs, ys, tensors, tok, stream_count, width, units, nc, cc)
+    plan = (zs, ys, tensors, units // nc, nc, width // cc, cc, stream_count * width * tensors)
+    bias = jnp.pad(mix_bias, (0, 128 - mix_bias.shape[0]))[None, :]
+    vmem = pl.BlockSpec(memory_space=pltpu.VMEM)
+    hbm = pl.BlockSpec(memory_space=pl.ANY)
+    out = pl.pallas_call(
+        functools.partial(layer_kernel, plan),
+        out_shape=jax.ShapeDtypeStruct((stream_count, tok, width), jnp.bfloat16),
+        in_specs=[vmem, vmem, vmem, hbm, hbm, hbm],
+        out_specs=vmem,
+        scratch_shapes=[pltpu.VMEM(shape, kind) for shape, kind in arrays]
+        + [pltpu.SemaphoreType.DMA(shape) for shape in sems],
+        compiler_params=pltpu.CompilerParams(
+            collective_id=0, has_side_effects=True, vmem_limit_bytes=VMEM_BUDGET
+        ),
+    )(streams.transpose(1, 0, 2), mix_weight.transpose(1, 0, 2), bias, gate_weight, up_weight, down_weight)
+    return out.transpose(1, 0, 2)
+
+
+def fits(mesh, streams, mix_weight, gate_weight):
+    tok, stream_count, width = streams.shape
+    units = gate_weight.shape[0]
+    dps, tensors = mesh.shape["dp"], mesh.shape["tensor"]
+    if dps % PAIR or tensors % PAIR or dps < 2 * PAIR or tensors < 2 * PAIR:
+        return False
+    zs, ys = dps // PAIR, tensors // PAIR
+    if units % UNIT_CHUNK or width % COLUMN_CHUNK or tok % 16 or (zs * tok) % (16 * ys):
+        return False
+    if mix_weight.shape[0] > 128:
+        return False
+    size = layer_scratch(zs, ys, tensors, tok, stream_count, width, units, UNIT_CHUNK, COLUMN_CHUNK)[2]
+    return size < VMEM_BUDGET * 3 // 4
+
+
 def solution(mesh):
     in_specs = (
         P("dp", None, "tensor"),
@@ -79,6 +509,11 @@
         P("dp", "tensor"),
     )
     out_specs = P("dp", None, "tensor")
-    return jax.shard_map(
-        per_device, mesh=mesh, in_specs=in_specs, out_specs=out_specs, check_vma=False
-    )
+
+    def step(streams, mix_weight, mix_bias, gate_weight, up_weight, down_weight):
+        operands = (streams, mix_weight, mix_bias, gate_weight, up_weight, down_weight)
+        if fits(mesh, streams, mix_weight, gate_weight):
+            return fused(mesh, *operands)
+        return per_device(*operands)
+
+    return jax.shard_map(step, mesh=mesh, in_specs=in_specs, out_specs=out_specs, check_vma=False)

time: 183 us -> 67.3 us (0.37)
  waiting for transfers between devices: 95.6 us -> 0 us
  Pallas kernels: 0 us -> 60.7 us
  blocking collectives: 47.5 us -> 0 us
  matrix products: 19.4 us -> 0 us
  between operations: 13.5 us -> 0.01 us
  other arithmetic: 6.14 us -> 0 us
  local copies, waits for them, and re-layouts: 0.28 us -> 6.32 us
    reduce_scatter x2 -> x0, waiting for transfers between devices: 95.6 us -> none  [the longest x1 63.1 us: per_device(): lax.psum_scatter(lax.dot_general(hidden, down_weight, (((0,), (0,)), ((),...]
    pallas_call x0 -> x1, Pallas kernels: none -> 60.7 us  [fused(): pl.pallas_call(functools.partial(layer_kernel, plan), out_shape=jax.Shape...]
    all_gather x2 -> x0, blocking collectives: 38.7 us -> none  [the longest x1 31.8 us: per_device(): block_rows = lax.all_gather(mlp_input, 'dp', axis=0, tiled=True)]
    dot_general x6 -> x0, matrix products: 19.4 us -> none  [the longest x2 8.91 us: contract_last(): lax.dot_general(weights, rows, (((1,), (1,)), ((), ())), preferred_elemen...]
    psum x1 -> x0, blocking collectives: 8.71 us -> none  [per_device(): total_logits, total_squares = lax.psum((raw_logits, squares), 'tensor')]
    unnamed x6 -> x2, local copies, waits for them, and re-layouts: 0.01 us -> 3.38 us
    reduce_sum x41 -> x0, other arithmetic: 2.03 us -> none  [the longest x1 1.22 us: per_device(): squares = jnp.sum(stream_wide * stream_wide, axis=(1, 2))]
  transfers between devices with their start and end apart: 2 -> 0, of which waited for: 2 -> 0; matrix products, arithmetic and copies ran while one was open for 1% -> 0% of each run, Pallas kernels for 0% -> 0%
where the time goes in v1:
time: 67.3 us; the launch traced here: 67.1 us
  Pallas kernels  60.7 us (90%)
  local copies, waits for them, and re-layouts  6.32 us (9%)
    pallas_call x1, Pallas kernels, fused(): pl.pallas_call(functools.partial(layer_kernel, plan), out_shape=jax.Shape...  60.7 us
    unnamed x2, local copies, waits for them, and re-layouts  3.38 us
    transpose x1, local copies, waits for them, and re-layouts, fused(): return out.transpose(1, 0, 2)  1.75 us

profile of v1, /device:TPU:0, one launch (start us, length us, event | category | flops | bytes accessed | tf_op | source)
XLA Modules:
  0.0 67.1 jit_solution(15759658047072753466)
XLA Ops:
  0.0 1.2 %pad_bitcast_fusion.bias_ref = f32[1,128]{1,0:T(1,128)} fusion(f32[24]{0:T(128)} %param.8), kind=kLoop, calls=%fused_computation.2 | loop fusion | bytes 608 | tf_op jit(solution)/shard_map/broadcast_in_dim | solution.py:470
  1.2 1.6 %copy.13 = bf16[16,4,1792]{2,0,1:T(8,128)(2,1)} copy(bf16[16,4,1792]{2,1,0:T(4,128)(2,1)} %param.6) | data formatting | bytes 458752 | tf_op args[0]
  2.8 1.7 %copy.12 = bf16[24,4,1792]{2,0,1:T(8,128)(2,1)} copy(bf16[24,4,1792]{2,1,0:T(4,128)(2,1)} %param.7) | data formatting | bytes 688128 | tf_op args[1]
  4.6 60.7 %shard_map.64 = bf16[4,16,1792]{2,1,0:T(8,128)(2,1)} custom-call(bf16[4,16,1792]{2,1,0:T(8,128)(2,1)} %bitcast.11, bf16[4,24,1792]{2,1,0:T(8,128)(2,1)} %bitcast.9, f32[1,128]{1,0:T(1,128)} %pad_bitcast_fusion.bias_ref, bf16[2304,1792]{1,0:T(8,128)(2,1)} %gate_hbm.1, bf16[2304,1792]{1,0:T(8,128)(2,1)} %up_hbm.1, bf16[2304,1792]{1,0:T(8,128)(2,1)} %down_hbm.1), custom_call_target="tpu_custom_call" | custom-call | tf_op jit(solution)/shard_map/pallas_call | solution.py:473
  65.3 1.7 %copy.9 = bf16[16,4,1792]{2,1,0:T(4,128)(2,1)} copy(bf16[16,4,1792]{2,0,1:T(8,128)(2,1)} %bitcast.10) | data formatting | bytes 458752 | tf_op jit(solution)/shard_map/transpose | solution.py:484

commit v2 on v1

--- a/solution.py
+++ b/solution.py
@@ -78,6 +78,8 @@
 UNIT_CHUNK = 256
 COLUMN_CHUNK = 256
 PAIR = 2
+GROUP = 3
+D_LAG = 4
 VMEM_BUDGET = 58 * 1024 * 1024
 
 
@@ -91,8 +93,8 @@
 
 def layer_kernel(
     plan,
-    s_ref,
-    mw_ref,
+    s_hbm,
+    mw_hbm,
     bias_ref,
     gate_hbm,
     up_hbm,
@@ -101,13 +103,16 @@
     gate_v,
     up_v,
     down_v,
+    s_raw,
+    mw_raw,
+    s_ref,
+    mw_ref,
     part,
     part_in,
     post,
     rows_all,
     mixed,
     sums,
-    pair_out,
     pair_in,
     pair_sum,
     ring_out,
@@ -119,6 +124,7 @@
     cross_sum,
     line_out,
     line_in,
+    in_sem,
     w_sem,
     a_send,
     a_recv,
@@ -181,13 +187,24 @@
         weight_copy(k, 2).start()
         return 0
 
-    lax.fori_loop(0, chunks, start_gate_up, 0)
-    lax.fori_loop(0, chunks, start_down, 0)
-
     barrier = pltpu.get_barrier_semaphore()
     peers = [t_peer(r) for r in range(1, tensors)] + [x_peer] + [z_peer(r) for r in range(1, zs)]
     for peer in peers:
         pl.semaphore_signal(barrier, inc=1, device_id=peer, device_id_type=MESH)
+
+    inputs = (
+        pltpu.make_async_copy(s_hbm, s_raw, in_sem.at[0]),
+        pltpu.make_async_copy(mw_hbm, mw_raw, in_sem.at[1]),
+    )
+    for copy in inputs:
+        copy.start()
+    lax.fori_loop(0, chunks, start_gate_up, 0)
+    lax.fori_loop(0, chunks, start_down, 0)
+    for copy in inputs:
+        copy.wait()
+    for j in range(streams):
+        s_ref[j] = s_raw[:, j, :]
+        mw_ref[j] = mw_raw[:, j, :]
 
     raw = jnp.zeros((tok, mw_ref.shape[1]), jnp.float32)
     squares = jnp.zeros((tok, 1), jnp.float32)
@@ -195,9 +212,9 @@
         raw += contract_last(s_ref[j], mw_ref[j])
         wide = s_ref[j].astype(jnp.float32)
         squares += jnp.sum(wide * wide, axis=1, keepdims=True)
-    part[0] = jnp.zeros((tok, part.shape[2]), jnp.float32)
-    part[0, :, : raw.shape[1]] = raw
-    part[1] = jnp.broadcast_to(squares, (tok, part.shape[2]))
+    count = raw.shape[1]
+    part[...] = jnp.broadcast_to(squares, part.shape)
+    part[:, :count] = raw
     pl.semaphore_wait(barrier, len(peers))
 
     def a_copy(r):
@@ -210,8 +227,8 @@
     total = part[...]
     for r in range(1, tensors):
         total = total + part_in[r - 1]
-    scale_inv = lax.rsqrt(total[1] / width_all + epsilon)
-    logits = total[0] * scale_inv + bias_ref[...]
+    scale_inv = lax.rsqrt(column(total, count) / width_all + epsilon)
+    logits = total[:, :count] * scale_inv + bias_ref[...]
     gates = sigmoid(logits)
     mlp_input = column(gates, 0) * s_ref[0].astype(jnp.float32)
     for j in range(1, streams):
@@ -253,10 +270,12 @@
         return tuple(m)
 
     order = sorted(range(1, zs), key=lambda r: min(r, zs - r))
+    share = ITERS // zs
     for r in order:
+        mat = lax.fori_loop(0, share, sweep, mat)
         send(rows_all.at[z], rows_all.at[z_at(-r)], bz_send.at[r - 1], bz_recv.at[r - 1], z_peer(r)).wait_recv()
         bx_copy(r).start()
-    mat = lax.fori_loop(0, ITERS, sweep, mat)
+    mat = lax.fori_loop(0, ITERS - share * len(order), sweep, mat)
     for i in range(streams):
         line = mat[i * streams] * s_ref[0].astype(jnp.float32)
         for j in range(1, streams):
@@ -270,13 +289,16 @@
     for r in range(zs):
         bx_arrival(r).wait_recv()
 
+    prod[...] = jnp.zeros_like(prod)
+    group = GROUP if chunks % GROUP == 0 else 1
+
     tokens = PAIR * zs * tok
     half = tokens // PAIR
     quarter = half // ys
     own_slot = core * ys + y
 
     def c1_copy(k):
-        return send(pair_out.at[k], pair_in.at[k], c1_send.at[k], c1_recv.at[k], core_peer)
+        return send(sums.at[k, 1 - core], pair_in.at[k], c1_send.at[k], c1_recv.at[k], core_peer)
 
     def c2_copy(k, r):
         at = (k * (ys - 1)) + r - 1
@@ -311,12 +333,11 @@
         rows = rows_all[...].reshape(tokens, width)
         sums[k, :, :, :nc] = contract_last(rows, gate_v[pl.ds(k * nc, nc)]).reshape(PAIR, half, nc)
         sums[k, :, :, nc:] = contract_last(rows, up_v[pl.ds(k * nc, nc)]).reshape(PAIR, half, nc)
-        pair_out[k] = sums[k, 1 - core].astype(jnp.bfloat16)
         c1_copy(k).start()
 
     def c_second(k):
         c1_copy(k).wait_recv()
-        both = sums[k, core] + pair_in[k].astype(jnp.float32)
+        both = sums[k, core] + pair_in[k]
         pair_sum[k] = both.reshape(ys, quarter, PAIR * nc)
         for r in range(1, ys):
             ring_out[k * (ys - 1) + r - 1] = pair_sum[k, y_at(r)].astype(jnp.bfloat16)
@@ -351,15 +372,28 @@
 
         lax.fori_loop(0, count + last, step, 0)
 
-    pipeline(chunks, ((0, c_first), (2, c_second), (4, c_third), (6, c_fourth)))
-
-    def finish_c(k, _):
+    def cols(n):
+        return pl.ds(pl.multiple_of(n * cc, cc), cc)
+
+    def down_piece(first, n):
+        span = pl.ds(pl.multiple_of(first * nc, nc), group * nc)
+        rows = hidden[:, :, span].reshape(tokens, group * nc)
+        return jnp.dot(rows, down_v[span, cols(n)], preferred_element_type=jnp.float32)
+
+    def c_fifth(k):
         for r in range(ys):
             c4_arrival(k, r).wait_recv()
         weight_copy(k, 2).wait()
-        return 0
-
-    lax.fori_loop(0, chunks, finish_c, 0)
+
+        @pl.when(jnp.logical_and(lax.rem(k, group) == group - 1, k < chunks - group))
+        def _():
+            def add(n, _):
+                prod[n] = prod[n] + down_piece(k - (group - 1), n)
+                return 0
+
+            lax.fori_loop(0, columns, add, 0)
+
+    pipeline(chunks, ((0, c_first), (2, c_second), (5, c_third), (8, c_fourth), (10, c_fifth)))
 
     def d1_copy(n):
         return send(cross_out.at[n], cross_in.at[n], d1_send.at[n], d1_recv.at[n], x_peer)
@@ -368,19 +402,15 @@
         at = n * (zs - 1) + r - 1
         return send(line_out.at[at], line_in.at[at], d2_send.at[at], d2_recv.at[at], z_peer(r))
 
-    def cols(n):
-        return pl.ds(pl.multiple_of(n * cc, cc), cc)
-
     def d_first(n):
-        rows = hidden[...].reshape(tokens, hidden.shape[2])
-        product = jnp.dot(rows, down_v[:, cols(n)], preferred_element_type=jnp.float32)
-        prod[n] = product[:half]
+        product = prod[n] + down_piece(chunks - group, n)
+        prod[n, :half] = product[:half]
         cross_out[n] = product[half:].astype(jnp.bfloat16)
         d1_copy(n).start()
 
     def d_second(n):
         d1_copy(n).wait_recv()
-        cross_sum[n] = (prod[n] + cross_in[n].astype(jnp.float32)).reshape(zs, tok, cc)
+        cross_sum[n] = (prod[n, :half] + cross_in[n].astype(jnp.float32)).reshape(zs, tok, cc)
         for r in range(1, zs):
             line_out[n * (zs - 1) + r - 1] = cross_sum[n, z_at(r)].astype(jnp.bfloat16)
             d2_copy(n, r).start()
@@ -393,7 +423,7 @@
         for i in range(streams):
             out_ref[i, :, cols(n)] = (mixed[i, :, cols(n)] + column(post[i], 0) * mlp_out).astype(jnp.bfloat16)
 
-    pipeline(columns, ((0, d_first), (1, d_second), (3, d_third)))
+    pipeline(columns, ((0, d_first), (D_LAG, d_second), (2 * D_LAG, d_third)))
 
     for r in range(1, tensors):
         a_copy(r).wait_send()
@@ -421,7 +451,7 @@
     lax.fori_loop(0, columns, drain_d, 0)
 
 
-def layer_scratch(zs, ys, tensors, tok, streams, width, units, nc, cc):
+def layer_scratch(zs, ys, tensors, tok, streams, logits, width, units, nc, cc):
     tokens = PAIR * zs * tok
     half = tokens // PAIR
     quarter = half // ys
@@ -432,19 +462,22 @@
         ((units, width), bf16),
         ((units, width), bf16),
         ((units, width), bf16),
-        ((2, tok, lanes), f32),
-        ((tensors - 1, 2, tok, lanes), f32),
+        ((tok, streams, width), bf16),
+        ((logits, streams, width), bf16),
+        ((streams, tok, width), bf16),
+        ((streams, logits, width), bf16),
+        ((tok, lanes), f32),
+        ((tensors - 1, tok, lanes), f32),
         ((streams, tok, lanes), f32),
         ((PAIR * zs, tok, width), bf16),
         ((streams, tok, width), f32),
         ((chunks, PAIR, half, 2 * nc), f32),
-        ((chunks, half, 2 * nc), bf16),
-        ((chunks, half, 2 * nc), bf16),
+        ((chunks, half, 2 * nc), f32),
         ((chunks, ys, quarter, 2 * nc), f32),
         ((chunks * (ys - 1), quarter, 2 * nc), bf16),
         ((chunks * (ys - 1), quarter, 2 * nc), bf16),
         ((PAIR * ys, quarter, units), bf16),
-        ((columns, half, cc), f32),
+        ((columns, tokens, cc), f32),
         ((columns, half, cc), bf16),
         ((columns, half, cc), bf16),
         ((columns, zs, tok, cc), f32),
@@ -452,7 +485,7 @@
         ((columns * (zs - 1), tok, cc), bf16),
     ]
     both = lambda count: [(count,), (count,)]
-    sems = [(3, chunks)]
+    sems = [(2,), (3, chunks)]
     for count in (tensors - 1, zs - 1, zs, chunks, chunks * (ys - 1), chunks * (ys - 1), chunks * ys, columns, columns * (zs - 1)):
         sems += both(count)
     size = sum(math.prod(shape) * jnp.dtype(kind).itemsize for shape, kind in arrays)
@@ -465,22 +498,22 @@
     dps, tensors = mesh.shape["dp"], mesh.shape["tensor"]
     zs, ys = dps // PAIR, tensors // PAIR
     nc, cc = UNIT_CHUNK, COLUMN_CHUNK
-    arrays, sems, _ = layer_scratch(zs, ys, tensors, tok, stream_count, width, units, nc, cc)
+    arrays, sems, _ = layer_scratch(zs, ys, tensors, tok, stream_count, mix_weight.shape[0], width, units, nc, cc)
     plan = (zs, ys, tensors, units // nc, nc, width // cc, cc, stream_count * width * tensors)
-    bias = jnp.pad(mix_bias, (0, 128 - mix_bias.shape[0]))[None, :]
+    bias = mix_bias[None, :]
     vmem = pl.BlockSpec(memory_space=pltpu.VMEM)
     hbm = pl.BlockSpec(memory_space=pl.ANY)
     out = pl.pallas_call(
         functools.partial(layer_kernel, plan),
         out_shape=jax.ShapeDtypeStruct((stream_count, tok, width), jnp.bfloat16),
-        in_specs=[vmem, vmem, vmem, hbm, hbm, hbm],
+        in_specs=[hbm, hbm, vmem, hbm, hbm, hbm],
         out_specs=vmem,
         scratch_shapes=[pltpu.VMEM(shape, kind) for shape, kind in arrays]
         + [pltpu.SemaphoreType.DMA(shape) for shape in sems],
         compiler_params=pltpu.CompilerParams(
             collective_id=0, has_side_effects=True, vmem_limit_bytes=VMEM_BUDGET
         ),
-    )(streams.transpose(1, 0, 2), mix_weight.transpose(1, 0, 2), bias, gate_weight, up_weight, down_weight)
+    )(streams, mix_weight, bias, gate_weight, up_weight, down_weight)
     return out.transpose(1, 0, 2)
 
 
@@ -493,9 +526,11 @@
     zs, ys = dps // PAIR, tensors // PAIR
     if units % UNIT_CHUNK or width % COLUMN_CHUNK or tok % 16 or (zs * tok) % (16 * ys):
         return False
-    if mix_weight.shape[0] > 128:
+    if mix_weight.shape[0] >= 128:
         return False
-    size = layer_scratch(zs, ys, tensors, tok, stream_count, width, units, UNIT_CHUNK, COLUMN_CHUNK)[2]
+    size = layer_scratch(
+        zs, ys, tensors, tok, stream_count, mix_weight.shape[0], width, units, UNIT_CHUNK, COLUMN_CHUNK
+    )[2]
     return size < VMEM_BUDGET * 3 // 4
 
 

time: 67.3 us -> 54.8 us (0.81)
  Pallas kernels: 60.7 us -> 52.9 us
  local copies, waits for them, and re-layouts: 6.32 us -> 1.75 us
    pallas_call x1, Pallas kernels: 60.7 us -> 52.9 us  [fused(): pl.pallas_call(functools.partial(layer_kernel, plan), out_shape=jax.Shape...]
    unnamed x2 -> x0, local copies, waits for them, and re-layouts: 3.38 us -> none
    broadcast_in_dim x1 -> x0, local copies, waits for them, and re-layouts: 1.2 us -> none  [fused(): bias = jnp.pad(mix_bias, (0, 128 - mix_bias.shape[0]))[None, :]]
where the time goes in v2:
time: 54.8 us; the launch traced here: 54.7 us
  Pallas kernels  52.9 us (97%)
  local copies, waits for them, and re-layouts  1.75 us (3%)
    pallas_call x1, Pallas kernels, fused(): pl.pallas_call(functools.partial(layer_kernel, plan), out_shape=jax.Shape...  52.9 us
    transpose x1, local copies, waits for them, and re-layouts, fused(): return out.transpose(1, 0, 2)  1.75 us

profile of v2, /device:TPU:0, one launch (start us, length us, event | category | flops | bytes accessed | tf_op | source)
XLA Modules:
  0.0 54.7 jit_solution(9407851145564147960)
XLA Ops:
  0.0 52.9 %shard_map.64 = bf16[4,16,1792]{2,1,0:T(8,128)(2,1)} custom-call(bf16[16,4,1792]{2,1,0:T(4,128)(2,1)} %s_hbm.1, bf16[24,4,1792]{2,1,0:T(4,128)(2,1)} %mw_hbm.1, f32[1,24]{1,0:T(1,128)} %bitcast.3, bf16[2304,1792]{1,0:T(8,128)(2,1)} %gate_hbm.1, bf16[2304,1792]{1,0:T(8,128)(2,1)} %up_hbm.1, bf16[2304,1792]{1,0:T(8,128)(2,1)} %down_hbm.1), custom_call_target="tpu_custom_call" | custom-call | tf_op jit(solution)/shard_map/pallas_call | solution.py:506
  52.9 1.7 %copy.7 = bf16[16,4,1792]{2,1,0:T(4,128)(2,1)} copy(bf16[16,4,1792]{2,0,1:T(8,128)(2,1)} %bitcast.2) | data formatting | bytes 458752 | tf_op jit(solution)/shard_map/transpose | solution.py:517
